TPU v7x, 256 devices: a whole 4x4x8 slice. The times are simulated.
256 devices in a mesh: seq: 32 (over x, z), chan: 8 (over y, core).
Axes of the slice: x: 4, y: 4, z: 8, core: 2. Of those that a mesh axis runs over, the one named last changes fastest.
Arguments:
- x_in: bfloat16 [24576, 5120], P('seq', 'chan'), may hold values from -120 to 120
- z_gate: bfloat16 [24576, 5120], P('seq', 'chan'), may hold values from -6 to 6
- b_proj: bfloat16 [24576, 128], P('seq'), may hold values from -6 to 6
- c_proj: bfloat16 [24576, 128], P('seq'), may hold values from -6 to 6
- dt_step: float32 [80, 24576], P('chan', 'seq'), may hold values from 0 to 1
- a_log: float32 [80], P('chan'), may hold values from -0.35 to 0.35
- skip_gain: float32 [80], P('chan'), may hold values from 0.5 to 1.5
- norm_gain: float32 [5120], P('chan'), may hold values from 0.5 to 1.5
- out_weight: bfloat16 [2560, 5120], P('seq', 'chan'), may hold values from -0.078125 to 0.078125
- out_grad: bfloat16 [24576, 2560], P('seq'), may hold values from -6 to 6
Outputs:
- d_x: bfloat16 [24576, 5120], P('seq', 'chan')
- d_z: bfloat16 [24576, 5120], P('seq', 'chan')
- d_dt: float32 [80, 24576], P('chan', 'seq')
- d_out_weight: float32 [2560, 5120], P('seq', 'chan')
All inputs are finite; a program needn't handle non-finite values.
Results may differ from a plain program's by a relative error of at most 0.005.
Values may be sent and summed in bfloat16 or wider, within the bound.
No kernel may reach another device: no remote copies, remote signals or barrier semaphores. Data moves between devices by JAX's collectives and lax.ppermute only.
A program may use at most 128 MiB of HBM per device.

v0:
```python
from functools import partial

import jax
import jax.numpy as jnp
from jax import lax
from jax.sharding import Mesh
from jax.sharding import PartitionSpec as P

GROUP = 256
SEQ = ("seq_0", "seq_1")


norm_eps = 1e-05
highest = lax.Precision.HIGHEST


def neutral_like(value, identity):
    return jax.tree.map(
        lambda part, zero: jnp.zeros_like(part) + jnp.asarray(zero, part.dtype), value, identity
    )


def carried_in(value, axes, combine, identity, reverse):
    before = start = neutral_like(value, identity)
    running = value
    for axis in reversed(axes):
        peers, index = (lax.axis_size(axis), lax.axis_index(axis))
        pieces = jax.tree.map(lambda part: lax.all_gather(part, axis), running)
        inside, running = (start, start)
        for k in reversed(range(peers)) if reverse else range(peers):
            passed = k > index if reverse else k < index
            running = combine(running, jax.tree.map(lambda part: part[k], pieces))
            inside = jax.tree.map(lambda new, old: jnp.where(passed, new, old), running, inside)
        before = combine(inside, before)
    return before


def joined_along(parts, dim):
    parts = jnp.moveaxis(parts, 0, dim)
    shape = parts.shape
    return parts.reshape(*shape[:dim], shape[dim] * shape[dim + 1], *shape[dim + 2 :])


def gather_in_order(value, axes, turns):
    parts = value
    for k in turns:
        parts = lax.all_gather(parts, axes[k])
    done = turns[::-1]
    back = [done.index(k) for k in range(len(axes))]
    parts = parts.transpose(*back, *range(len(axes), parts.ndim))
    return parts.reshape(-1, *value.shape)


def gathered_by_axis(value, axes, turns, dim):
    return joined_along(gather_in_order(value, axes, turns), dim)


def from_everyone(value, axis):
    peers = lax.axis_size(axis)
    return lax.all_to_all(
        jnp.broadcast_to(value[None], (peers, *value.shape)), axis, 0, 0, tiled=True
    )


def taken_together(value, axis):
    everything = from_everyone(value, axis)
    return jnp.sum(everything, axis=0)


def in_blocks(value, dim, peers):
    before, after = (value.shape[:dim], value.shape[dim + 1 :])
    return jnp.moveaxis(value.reshape(*before, peers, -1, *after), dim, 0)


def sum_at_owner(value, axis, dim):
    parts = in_blocks(value, dim, lax.axis_size(axis))
    arrived = lax.all_to_all(parts, axis, split_axis=0, concat_axis=0, tiled=True)
    return arrived.astype(jnp.float32).sum(axis=0)


def group_step(state_in, pieces, decay_rates, skip_gain):
    x_part, dt_part, b_part, c_part = pieces
    log_decay = jnp.cumsum(-decay_rates[:, None] * dt_part, axis=1)
    length = dt_part.shape[1]
    row_ids = lax.broadcasted_iota(jnp.int32, (length, length), 0)
    col_ids = lax.broadcasted_iota(jnp.int32, (length, length), 1)
    causal = (row_ids >= col_ids)[None]
    log_gap = jnp.where(causal, log_decay[:, :, None] - log_decay[:, None, :], 0.0)
    decay_mat = jnp.where(causal, jnp.exp(log_gap), 0.0)
    affinity = jnp.dot(c_part, b_part.T, precision=highest)
    weighted = x_part * jnp.transpose(dt_part)[:, :, None]
    within = jnp.einsum("hts,shp->thp", decay_mat * affinity[None], weighted, precision=highest)
    carried = jnp.transpose(jnp.exp(log_decay))[:, :, None] * jnp.einsum(
        "tn,hpn->thp", c_part, state_in, precision=highest
    )
    output = within + carried + skip_gain[None, :, None] * x_part
    to_end = jnp.exp(log_decay[:, -1:] - log_decay)
    update = jnp.einsum("shp,hs,sn->hpn", weighted, to_end, b_part, precision=highest)
    state_out = jnp.exp(log_decay[:, -1])[:, None, None] * state_in + update
    return (state_out, output)


def ssd_local(x_vals, dt_vals, b_vals, c_vals, decay_rates, skip_gain, state_in):
    length, head_count, head_size = x_vals.shape
    blocks = length // GROUP
    x_blocks = x_vals.reshape(blocks, GROUP, head_count, head_size)
    dt_blocks = jnp.transpose(dt_vals.reshape(head_count, blocks, GROUP), (1, 0, 2))
    b_blocks = b_vals.reshape(blocks, GROUP, -1)
    c_blocks = c_vals.reshape(blocks, GROUP, -1)
    stepper = jax.checkpoint(partial(group_step, decay_rates=decay_rates, skip_gain=skip_gain))
    state_out, outputs = lax.scan(stepper, state_in, (x_blocks, dt_blocks, b_blocks, c_blocks))
    return (outputs.reshape(length, head_count, head_size), state_out)


def combine_pair(earlier, later):
    return (earlier[0] * later[0], later[0][:, None, None] * earlier[1] + later[1])


def shards(
    x_in, z_gate, b_proj, c_proj, dt_step, a_log, skip_gain, norm_gain, out_weight, out_grad
):
    length, width = x_in.shape
    head_count = a_log.shape[0]
    head_size = width // head_count
    decay_rates = jnp.exp(a_log)
    b_vals = b_proj.astype(jnp.float32)
    c_vals = c_proj.astype(jnp.float32)
    zero_state = jnp.zeros((head_count, head_size, b_vals.shape[1]), jnp.float32)
    identity_pair = (jnp.ones((head_count,), jnp.float32), zero_state)

    def local_part(x_arg, dt_arg):
        return ssd_local(x_arg, dt_arg, b_vals, c_vals, decay_rates, skip_gain, zero_state)

    x_vals = x_in.astype(jnp.float32).reshape(length, head_count, head_size)
    (y_local, s_local), pull_local = jax.vjp(local_part, x_vals, dt_step)
    device_decay = jnp.exp(-decay_rates * jnp.sum(dt_step, axis=1))
    scanned = carried_in((device_decay, s_local), SEQ, combine_pair, identity_pair, False)
    state_in = scanned[1]

    def outside_part(dt_arg, state_arg):
        log_run = jnp.cumsum(-decay_rates[:, None] * dt_arg, axis=1)
        return jnp.transpose(jnp.exp(log_run))[:, :, None] * jnp.einsum(
            "tn,hpn->thp", c_vals, state_arg, precision=highest
        )

    y_outside, pull_outside = jax.vjp(outside_part, dt_step, state_in)
    y_vals = (y_local + y_outside).reshape(length, width)
    columns = out_grad
    grad_sum = jnp.dot(
        columns, gathered_by_axis(out_weight, SEQ, (0, 1), 0), preferred_element_type=jnp.float32
    )
    grad_norm = grad_sum.astype(jnp.bfloat16)
    z_vals = z_gate.astype(jnp.float32)
    sigmoid_z = jax.nn.sigmoid(z_vals)
    gate_act = z_vals * sigmoid_z
    gated_y = y_vals * gate_act
    full_width = width * lax.axis_size("chan")
    scaled_grad = grad_norm.astype(jnp.float32) * norm_gain
    local_squares = jnp.sum(gated_y * gated_y, axis=1)
    local_dots = jnp.sum(gated_y * scaled_grad, axis=1)
    square_sum, dot_sum = (
        taken_together(local_squares, "chan"),
        taken_together(local_dots, "chan"),
    )
    inverse_scale = lax.rsqrt(square_sum / full_width + norm_eps)
    normed = (gated_y * inverse_scale[:, None] * norm_gain).astype(jnp.bfloat16)
    columns = out_grad
    weight_grad = sum_at_owner(
        lax.dot_general(
            columns, normed, (((0,), (0,)), ((), ())), preferred_element_type=jnp.float32
        ).astype(jnp.bfloat16),
        SEQ,
        0,
    )
    grad_gated = (
        inverse_scale[:, None] * scaled_grad
        - gated_y * (inverse_scale**3 * dot_sum / full_width)[:, None]
    )
    grad_z = (grad_gated * y_vals * sigmoid_z * (1.0 + z_vals * (1.0 - sigmoid_z))).astype(
        jnp.bfloat16
    )
    grad_y = (grad_gated * gate_act).reshape(length, head_count, head_size)
    grad_dt_outside, grad_local = pull_outside(grad_y)
    scanned_back = carried_in((device_decay, grad_local), SEQ, combine_pair, identity_pair, True)
    grad_out = scanned_back[1]
    grad_x_vals, grad_dt_local = pull_local((grad_y, grad_out))
    grad_decay = jnp.sum(grad_out * state_in, axis=(1, 2))
    grad_dt = grad_dt_local + grad_dt_outside - (grad_decay * device_decay * decay_rates)[:, None]
    grad_x = grad_x_vals.reshape(length, width).astype(jnp.bfloat16)
    return (grad_x, grad_z, grad_dt, weight_grad)


def solution(mesh):
    torus = Mesh(mesh.devices.reshape(4, 8, mesh.shape["chan"]), ("seq_0", "seq_1", "chan"))
    return jax.shard_map(
        shards,
        mesh=torus,
        in_specs=(
            P(SEQ, "chan"),
            P(SEQ, "chan"),
            P(SEQ, None),
            P(SEQ, None),
            P("chan", SEQ),
            P("chan"),
            P("chan"),
            P("chan"),
            P(SEQ, "chan"),
            P(SEQ, None),
        ),
        out_specs=(P(SEQ, "chan"), P(SEQ, "chan"), P("chan", SEQ), P(SEQ, "chan")),
        check_vma=False,
    )
```

profile of v0, /device:TPU:1, one launch (start us, length us, event | category | flops | bytes accessed | tf_op | source)
XLA Modules:
  0.0 464.6 jit_solution(11437954571626023379)
XLA Ops:
  10.7 1.5 copy.144
  12.2 2.2 reshape.461
  14.3 3.5 copy.146
  17.9 75.7 %while.37 = (s32[]{:T(128)}, f32[10,64,128]{2,1,0:T(8,128)S(1)}, f32[3,256,10,64]{1,0,3,2:T(4,128)}, f32[3,10,64,128]{3,2,1,0:T(8,128)}, f32[10,1]{0,1:T(1,128)S...) while((s32[]{:T(128)}, f32[10,64,128]{2,1,0:T(8,128)S(1)}, ...), condition=%wide.region_6.7_spmd.clone.clone, body=%wide.region_3.6_spmd.clone.clone.sunk | while | flops 1111806976 | bytes 9664000 | solution.py:111
  20.3 4.4 fusion.197
  26.1 1.9 convolution_add_fusion.5
  28.0 15.1 %dynamic_update_slice.47 = f32[3,256,10,64]{1,0,3,2:T(4,128)} dynamic-update-slice(f32[3,256,10,64]{1,0,3,2:T(4,128)} %get-tuple-element.917, f32[1,256,10,64]{1,0,3,2:T(1,128)S(1)} %copy.217, s32[]{:T(128)S(6)} %copy.226, s32[]{:T(128)} %constant.122.clone.1..sunk, s32[]{:T(128)} %constant.122.clone.1..sunk, s32[]{:T(128)} %constant.122.clone.1..sunk) | dynamic-update-slice | bytes 1310724 | tf_op jit(solution)/shard_map/jvp()/while/body/jit(dynamic_update_index_in_dim)/dynamic_update_slice | solution.py:111
  45.5 4.4 fusion.197
  51.4 1.9 convolution_add_fusion.5
  53.3 15.1 %dynamic_update_slice.47 = f32[3,256,10,64]{1,0,3,2:T(4,128)} dynamic-update-slice(f32[3,256,10,64]{1,0,3,2:T(4,128)} %get-tuple-element.917, f32[1,256,10,64]{1,0,3,2:T(1,128)S(1)} %copy.217, s32[]{:T(128)S(6)} %copy.226, s32[]{:T(128)} %constant.122.clone.1..sunk, s32[]{:T(128)} %constant.122.clone.1..sunk, s32[]{:T(128)} %constant.122.clone.1..sunk) | dynamic-update-slice | bytes 1310724 | tf_op jit(solution)/shard_map/jvp()/while/body/jit(dynamic_update_index_in_dim)/dynamic_update_slice | solution.py:111
  70.7 4.4 fusion.197
  76.6 1.9 convolution_add_fusion.5
  78.5 15.1 %dynamic_update_slice.47 = f32[3,256,10,64]{1,0,3,2:T(4,128)} dynamic-update-slice(f32[3,256,10,64]{1,0,3,2:T(4,128)} %get-tuple-element.917, f32[1,256,10,64]{1,0,3,2:T(1,128)S(1)} %copy.217, s32[]{:T(128)S(6)} %copy.226, s32[]{:T(128)} %constant.122.clone.1..sunk, s32[]{:T(128)} %constant.122.clone.1..sunk, s32[]{:T(128)} %constant.122.clone.1..sunk) | dynamic-update-slice | bytes 1310724 | tf_op jit(solution)/shard_map/jvp()/while/body/jit(dynamic_update_index_in_dim)/dynamic_update_slice | solution.py:111
  94.4 12.4 %all-gather.2 = bf16[320,640]{1,0:T(8,128)(2,1)} all-gather(bf16[80,640]{1,0:T(8,128)(2,1)S(1)} %copy-done.14), channel_id=4, replica_groups=mesh['seq_0'=4,'seq_1'=8,'chan'=8] {'seq_0'}, dimensions={0}, use_global_device_ids=true | all-gather | bytes 512000 | tf_op jit(solution)/shard_map/all_gather | solution.py:47
  108.4 17.2 %all-reduce.2 = f32[80]{0:T(128)S(1)} all-reduce(f32[80]{0:T(128)S(1)} %fusion.139), channel_id=2, replica_groups=mesh['seq_0'=4,'seq_1'=8,'chan'=8] {'seq_1'}, use_global_device_ids=true, to_apply=%add.2 | all-reduce | flops 80 | bytes 640
  126.9 10.6 %all-gather.17.cloned.1.call-done = f32[80,64,128]{2,1,0:T(8,128)} async-done(((f32[10,64,128]{2,1,0:T(8,128)}), f32[80,64,128]{2,1,0:T(8,128)}) %all-gather.17.cloned.1.call-update) | async-done | bytes 2621456 | tf_op jit(solution)/shard_map/all_gather | solution.py:28
  137.5 2.7 bitcast_add_fusion.9
  140.9 3.3 reduce-window.78
  144.5 2.2 copy.148
  146.8 2.3 reshape.453
  149.2 8.4 %all-gather.6 = f32[4,1,10]{2,1,0:T(1,128)S(1)} all-gather(f32[1,1,10]{2,1,0:T(1,128)S(1)} %get-tuple-element.695), channel_id=1, replica_groups=mesh['seq_0'=4,'seq_1'=8,'chan'=8] {'seq_0'}, dimensions={0}, use_global_device_ids=true | all-gather | bytes 200 | tf_op jit(solution)/shard_map/all_gather | solution.py:28
  158.1 29.1 %all-gather.19.cloned.1.call-done = bf16[32,80,640]{2,1,0:T(8,128)(2,1)} async-done(((bf16[4,80,640]{2,1,0:T(8,128)(2,1)}), bf16[32,80,640]{2,1,0:T(8,128)(2,1)}) %all-gather.19.cloned.1.call-update) | async-done | bytes 3276816 | tf_op jit(solution)/shard_map/all_gather | solution.py:47
  187.2 4.1 copy.150
  191.3 22.7 %all-gather.13.cloned.1.call-done = f32[4,10,64,128]{3,2,1,0:T(8,128)} async-done(((f32[1,10,64,128]{3,2,1,0:T(8,128)}), f32[4,10,64,128]{3,2,1,0:T(8,128)}) %all-gather.13.cloned.1.call-update) | async-done | bytes 1310736 | tf_op jit(solution)/shard_map/all_gather | solution.py:28
  214.1 2.2 fusion.107
  216.4 2.3 fusion.89
  219.6 5.2 %multiply_reduce_fusion.3 = (f32[768]{0:T(1024)S(1)}, f32[768]{0:T(1024)S(1)}, f32[768,640]{0,1:T(8,128)}, bf16[768,640]{0,1:T(8,128)(2,1)}) fusion(f32[640]{0:T(1024)S(1)} %copy-done.33, bf16[768,640]{0,1:T(8,128)(2,1)S(1)} %copy-done.5, f32[768,10,64]{0,2,1:T(8,128)S(1)} %get-tuple-element.706, bf16[768,2560]{1,0:T(8,128)(2,1)S(1)} %copy-done.43, ...), kind=kOutput, calls=%fused_computation.135 | convolution fusion | flops 2522970624 | bytes 13115904 | tf_op jit(solution)/shard_map/dot_general | solution.py:149
  224.8 10.6 %all_to_all.17 = f32[8,1,768]{2,1,0:T(1,128)S(1)} all-to-all(f32[8,1,768]{2,1,0:T(1,128)S(1)} %broadcast_in_dim.159), channel_id=1, replica_groups=mesh['seq_0'=4,'seq_1'=8,'chan'=8] {'chan'}, dimensions={0} | all-to-all | bytes 49152 | tf_op jit(solution)/shard_map/all_to_all | solution.py:60
  235.9 4.0 all-to-all-start.1
  239.9 4.7 %all-to-all-done.1 = f32[8,1,768]{2,1,0:T(1,128)S(1)} async-done(((f32[8,1,768]{2,1,0:T(1,128)}), f32[8,1,768]{2,1,0:T(1,128)S(1)}, u32[]{:S(2)}, u32[]{:S(2)}) %all-to-all-start.1) | async-done | bytes 24608 | tf_op jit(solution)/shard_map/all_to_all | solution.py:60
  244.7 4.9 %fusion.87 = (bf16[768,640]{0,1:T(8,128)(2,1)}, f32[768,640]{0,1:T(8,128)S(1)}) fusion(bf16[768,640]{0,1:T(8,128)(2,1)} %copy.148, f32[768,10,64]{0,2,1:T(8,128)} %copy-done.3, f32[768,640]{0,1:T(8,128)} %get-tuple-element.658, bf16[768,640]{0,1:T(8,128)(2,1)} %get-tuple-element.708, f32[768]{0:T(1024)S(1)} %get-tuple-element.679, f32[640]{0:T(1024)S(1)} %copy-done.33, ...), kind=kLoop, calls=%fused_computation.121 | loop fusion | flops 8847360 | bytes 8856064 | tf_op jit(solution)/shard_map/convert_element_type | solution.py:179
  249.6 1.8 fusion.91
  251.4 7.2 %fusion.81 = bf16[2560,640]{0,1:T(8,128)(2,1)} fusion(bf16[768,2560]{1,0:T(8,128)(2,1)} %param.23, f32[768,640]{0,1:T(8,128)} %get-tuple-element.658, f32[640]{0:T(1024)S(1)} %copy-done.33, f32[768]{0:T(1024)S(1)} %get-tuple-element.678), kind=kOutput, calls=%fused_computation.112 | convolution fusion | flops 2519695360 | bytes 9180672 | tf_op jit(solution)/shard_map/dot_general | solution.py:169
  258.6 5.7 %copy.159 = bf16[2560,640]{1,0:T(8,128)(2,1)} copy(bf16[2560,640]{0,1:T(8,128)(2,1)} %fusion.81) | data formatting | bytes 6553600 | tf_op jit(solution)/shard_map/convert_element_type | solution.py:171
  264.3 9.2 %all-to-all-start.2 = ((bf16[32,80,640]{2,1,0:T(8,128)(2,1)}), bf16[32,80,640]{2,1,0:T(8,128)(2,1)}, u32[]{:S(2)}, u32[]{:S(2)}) async-start(bf16[32,80,640]{2,1,0:T(8,128)(2,1)} %bitcast.515), calls=%async_computation.2 | async-start | bytes 6553600 | tf_op jit(solution)/shard_map/all_to_all | solution.py:77
  273.5 48.6 %all-gather.21.cloned.1.call-done = f32[80,64,128]{2,1,0:T(8,128)} async-done(((f32[10,64,128]{2,1,0:T(8,128)}), f32[80,64,128]{2,1,0:T(8,128)}) %all-gather.21.cloned.1.call-update) | async-done | bytes 2621456 | tf_op jit(solution)/shard_map/all_gather | solution.py:28
  322.2 2.6 bitcast_add_fusion.1
  324.8 7.4 %all-gather.5 = f32[4,1,10]{2,1,0:T(1,128)S(1)} all-gather(f32[1,1,10]{2,1,0:T(1,128)S(1)} %get-tuple-element.694), channel_id=1, replica_groups=mesh['seq_0'=4,'seq_1'=8,'chan'=8] {'seq_0'}, dimensions={0}, use_global_device_ids=true | all-gather | bytes 200 | tf_op jit(solution)/shard_map/all_gather | solution.py:28
  332.3 2.2 reshape_reshape.15
  334.5 1.8 fusion.90
  336.4 2.2 copy.161
  338.6 7.5 %reduce-window.80 = f32[10,6,128]{2,0,1:T(8,128)S(1)} reduce-window(f32[10,6,128]{2,0,1:T(8,128)S(1)} %copy.157, f32[]{:T(128)} %constant.125.clone.1), window={size=1x1x128 pad=0_0x0_0x0_127}, to_apply=%region_24.25 | reduce-window | flops 975360 | bytes 61444 | tf_op jit(solution)/shard_map/reduce-window.6
  346.9 16.9 %all-to-all-done.2 = bf16[32,80,640]{2,1,0:T(8,128)(2,1)} async-done(((bf16[32,80,640]{2,1,0:T(8,128)(2,1)}), bf16[32,80,640]{2,1,0:T(8,128)(2,1)}, u32[]{:S(2)}, u32[]{:S(2)}) %all-to-all-start.2) | async-done | bytes 3276832 | tf_op jit(solution)/shard_map/all_to_all | solution.py:77
  363.9 3.1 convert_reduce_fusion
  367.0 2.7 all-gather.15.cloned.1.call-done
  369.7 2.8 multiply_reduce_fusion.4
  374.7 78.0 %while.36 = (s32[]{:T(128)}, f32[10,64,128]{2,1,0:T(8,128)S(1)}, bf16[3,256,10,64]{1,3,2,0:T(8,128)(2,1)}, f32[3,10,256]{2,1,0:T(8,128)}, f32[3,10,64,128]{3,2,1...) while((s32[]{:T(128)}, f32[10,64,128]{2,1,0:T(8,128)S(1)}, ...), condition=%wide.region_22.23_spmd, body=%wide.region_11.22_spmd.sunk | while | flops 1873505792 | bytes 18949208 | solution.py:111
  384.7 2.4 constant_dynamic-slice_fusion.4
  391.5 4.2 fusion.184
  397.5 2.5 reduce-window.94
  400.2 1.5 convolution_add_fusion.4
  401.7 4.1 bitcast_dynamic-update-slice_fusion.6
  407.7 2.4 constant_dynamic-slice_fusion.4
  414.5 4.2 fusion.184
  420.5 2.5 reduce-window.94
  423.3 1.5 convolution_add_fusion.4
  424.8 4.1 bitcast_dynamic-update-slice_fusion.6
  430.7 2.4 constant_dynamic-slice_fusion.4
  437.5 4.2 fusion.184
  443.5 2.5 reduce-window.94
  446.3 1.5 convolution_add_fusion.4
  447.8 4.1 bitcast_dynamic-update-slice_fusion.6
  453.6 2.0 copy.155
  455.9 1.3 copy.160
  (338 shorter events, 50.6 us)
Async XLA Ops:
  7.2 130.3 %all-gather.17.cloned.1.call-start = ((), (), s32[]{:S(2)}) async-start(), calls=%async_computation.5 | async-start | bytes 2949120 | tf_op jit(solution)/shard_map/all_gather | solution.py:28
  7.9 100.1 %copy-start.34 = (f32[10]{0:T(128)}, f32[10]{0:T(128)S(1)}, u32[]{:S(2)}) copy-start(f32[10]{0:T(128)S(1)} %get-tuple-element.700) | copy-start | bytes 124
  14.3 3.5 copy-start.44
  17.9 76.5 %copy-start.14 = (bf16[80,640]{1,0:T(8,128)(2,1)S(1)}, bf16[80,640]{1,0:T(8,128)(2,1)}, u32[]{:S(2)}) copy-start(bf16[80,640]{1,0:T(8,128)(2,1)} %param.22) | copy-start | bytes 307204
  17.9 89.0 %copy-start.45 = (u32[256]{0:T(256)S(1)}, u32[256]{0:T(256)}, u32[]{:S(2)}) copy-start(u32[256]{0:T(256)} %constant.147) | copy-start | bytes 3076
  17.9 90.2 %copy-start.13 = (f32[10,768]{1,0:T(8,128)S(1)}, f32[10,768]{1,0:T(8,128)}, u32[]{:S(2)}) copy-start(f32[10,768]{1,0:T(8,128)} %param.18) | copy-start | bytes 92164
  17.9 90.4 %copy-start.38 = (f32[10]{0:T(128)S(1)}, f32[10]{0:T(128)}, u32[]{:S(2)}) copy-start(f32[10]{0:T(128)} %param.19) | copy-start | bytes 124
  93.6 0.7 copy-start
  94.3 92.9 %all-gather.19.cloned.1.call-start = ((), (), s32[]{:S(2)}) async-start(), calls=%async_computation.6 | async-start | bytes 3686400 | tf_op jit(solution)/shard_map/all_gather | solution.py:47
  106.7 107.2 %all-gather.13.cloned.1.call-start = ((), (), s32[]{:S(2)}) async-start(), calls=%async_computation.3 | async-start | bytes 1638400 | tf_op jit(solution)/shard_map/all_gather | solution.py:28
  108.2 29.3 %copy-start.27 = (f32[10]{0:T(128)}, f32[10]{0:T(128)S(1)}, u32[]{:S(2)}) copy-start(f32[10]{0:T(128)S(1)} %get-tuple-element.677) | copy-start | bytes 124
  125.7 14.5 %copy-start.19 = (f32[10]{0:T(128)}, f32[10]{0:T(128)S(1)}, u32[]{:S(2)}) copy-start(f32[10]{0:T(128)S(1)} %get-tuple-element.702) | copy-start | bytes 124
  125.7 14.5 %copy-start.21 = (f32[10]{0:T(128)}, f32[10]{0:T(128)S(1)}, u32[]{:S(2)}) copy-start(f32[10]{0:T(128)S(1)} %get-tuple-element.703) | copy-start | bytes 124
  125.7 14.6 %copy-start.23 = (f32[10]{0:T(128)}, f32[10]{0:T(128)S(1)}, u32[]{:S(2)}) copy-start(f32[10]{0:T(128)S(1)} %get-tuple-element.704) | copy-start | bytes 124
  125.7 14.6 %copy-start.31 = (f32[10]{0:T(128)}, f32[10]{0:T(128)S(1)}, u32[]{:S(2)}) copy-start(f32[10]{0:T(128)S(1)} %get-tuple-element.705) | copy-start | bytes 124
  126.3 14.0 %copy-start.29 = (f32[10]{0:T(128)}, f32[10]{0:T(128)S(1)}, u32[]{:S(2)}) copy-start(f32[10]{0:T(128)S(1)} %get-tuple-element.692) | copy-start | bytes 124
  126.9 13.3 %copy-start.15 = (f32[10]{0:T(128)}, f32[10]{0:T(128)S(1)}, u32[]{:S(2)}) copy-start(f32[10]{0:T(128)S(1)} %get-tuple-element.698) | copy-start | bytes 124
  126.9 13.3 %copy-start.17 = (f32[10]{0:T(128)}, f32[10]{0:T(128)S(1)}, u32[]{:S(2)}) copy-start(f32[10]{0:T(128)S(1)} %get-tuple-element.699) | copy-start | bytes 124
  140.2 6.6 %copy-start.9 = (f32[3,256,10,64]{1,0,3,2:T(4,128)S(1)}, f32[3,256,10,64]{1,0,3,2:T(4,128)}, u32[]{:S(2)}) copy-start(f32[3,256,10,64]{1,0,3,2:T(4,128)} %get-tuple-element.385) | copy-start | bytes 5898244
  187.2 26.8 %copy-start.1 = (f32[80,64,128]{2,1,0:T(8,128)S(1)}, f32[80,64,128]{2,1,0:T(8,128)}, u32[]{:S(2)}) copy-start(f32[80,64,128]{2,1,0:T(8,128)} %all-gather.17.cloned.1.call-done) | copy-start | bytes 7864324
  187.2 26.8 %copy-start.16 = (f32[10]{0:T(128)S(1)}, f32[10]{0:T(128)}, u32[]{:S(2)}) copy-start(f32[10]{0:T(128)} %copy-done.15) | copy-start | bytes 124
  187.2 26.8 %copy-start.18 = (f32[10]{0:T(128)S(1)}, f32[10]{0:T(128)}, u32[]{:S(2)}) copy-start(f32[10]{0:T(128)} %copy-done.17) | copy-start | bytes 124
  187.2 26.8 %copy-start.20 = (f32[10]{0:T(128)S(1)}, f32[10]{0:T(128)}, u32[]{:S(2)}) copy-start(f32[10]{0:T(128)} %copy-done.19) | copy-start | bytes 124
  187.2 26.8 %copy-start.22 = (f32[10]{0:T(128)S(1)}, f32[10]{0:T(128)}, u32[]{:S(2)}) copy-start(f32[10]{0:T(128)} %copy-done.21) | copy-start | bytes 124
  187.2 26.8 %copy-start.24 = (f32[10]{0:T(128)S(1)}, f32[10]{0:T(128)}, u32[]{:S(2)}) copy-start(f32[10]{0:T(128)} %copy-done.23) | copy-start | bytes 124
  187.2 26.8 %copy-start.30 = (f32[10]{0:T(128)S(1)}, f32[10]{0:T(128)}, u32[]{:S(2)}) copy-start(f32[10]{0:T(128)} %copy-done.29) | copy-start | bytes 124
  187.2 26.8 %copy-start.32 = (f32[10]{0:T(128)S(1)}, f32[10]{0:T(128)}, u32[]{:S(2)}) copy-start(f32[10]{0:T(128)} %copy-done.31) | copy-start | bytes 124
  187.2 26.8 %copy-start.40 = (f32[10]{0:T(128)S(1)}, f32[10]{0:T(128)}, u32[]{:S(2)}) copy-start(f32[10]{0:T(128)} %get-tuple-element.697) | copy-start | bytes 124
  214.0 2.3 copy-start.2
  214.1 2.3 copy-start.10
  214.1 4.6 copy-start.43
  216.3 2.3 copy-start.7
  216.3 2.3 copy-start.5
  216.3 3.2 copy-start.6
  216.3 3.2 copy-start.33
  218.6 6.1 %copy-start.3 = (f32[768,10,64]{0,2,1:T(8,128)}, f32[768,10,64]{0,2,1:T(8,128)S(1)}, u32[]{:S(2)}) copy-start(f32[768,10,64]{0,2,1:T(8,128)S(1)} %get-tuple-element.706) | copy-start | bytes 5898244
  235.9 8.7 %all-to-all-start.1 = ((f32[8,1,768]{2,1,0:T(1,128)}), f32[8,1,768]{2,1,0:T(1,128)S(1)}, u32[]{:S(2)}, u32[]{:S(2)}) async-start(f32[8,1,768]{2,1,0:T(1,128)} %broadcast_in_dim.160), calls=%async_computation.1 | async-start | bytes 49152 | tf_op jit(solution)/shard_map/all_to_all | solution.py:60
  239.9 82.2 %all-gather.21.cloned.1.call-start = ((), (), s32[]{:S(2)}) async-start(), calls=%async_computation.7 | async-start | bytes 2949120 | tf_op jit(solution)/shard_map/all_gather | solution.py:28
  244.7 4.9 %copy-start.11 = (bf16[768,128]{1,0:T(8,128)(2,1)S(1)}, bf16[768,128]{1,0:T(8,128)(2,1)}, u32[]{:S(2)}) copy-start(bf16[768,128]{1,0:T(8,128)(2,1)} %param.17) | copy-start | bytes 589828
  264.3 57.9 %copy-start.25 = (f32[10]{0:T(128)S(1)}, f32[10]{0:T(128)}, u32[]{:S(2)}) copy-start(f32[10]{0:T(128)} %get-tuple-element.691) | copy-start | bytes 124
  264.3 57.9 %copy-start.26 = (f32[10]{0:T(128)S(1)}, f32[10]{0:T(128)}, u32[]{:S(2)}) copy-start(f32[10]{0:T(128)} %get-tuple-element.696) | copy-start | bytes 124
  264.3 99.6 %all-to-all-start.2 = ((bf16[32,80,640]{2,1,0:T(8,128)(2,1)}), bf16[32,80,640]{2,1,0:T(8,128)(2,1)}, u32[]{:S(2)}, u32[]{:S(2)}) async-start(bf16[32,80,640]{2,1,0:T(8,128)(2,1)} %bitcast.515), calls=%async_computation.2 | async-start | bytes 6553600 | tf_op jit(solution)/shard_map/all_to_all | solution.py:77
  273.5 96.2 %all-gather.15.cloned.1.call-start = ((), (), s32[]{:S(2)}) async-start(), calls=%async_computation.4 | async-start | bytes 1638400 | tf_op jit(solution)/shard_map/all_gather | solution.py:28
  346.2 23.6 %copy-start.8 = (f32[10,64,128]{2,1,0:T(8,128)S(1)}, f32[10,64,128]{2,1,0:T(8,128)}, u32[]{:S(2)}) copy-start(f32[10,64,128]{2,1,0:T(8,128)} %copy-done.7) | copy-start | bytes 983044
  346.2 23.6 %copy-start.36 = (f32[10]{0:T(128)S(1)}, f32[10]{0:T(128)}, u32[]{:S(2)}) copy-start(f32[10]{0:T(128)} %get-tuple-element.690) | copy-start | bytes 124
  369.7 2.8 copy-start.28
  369.7 2.8 copy-start.39
  383.6 4.7 %copy-start.41 = (f32[10]{0:T(128)}, f32[10]{0:T(128)S(1)}, u32[]{:S(2)}) copy-start(f32[10]{0:T(128)S(1)} %get-tuple-element.870) | copy-start | bytes 124 | tf_op jit(solution)/shard_map/transpose(jvp())/while
  391.4 4.2 copy-start.4
  401.7 4.9 %copy-start.42 = (f32[10]{0:T(128)S(1)}, f32[10]{0:T(128)}, u32[]{:S(2)}) copy-start(f32[10]{0:T(128)} %copy-done.41) | copy-start | bytes 124 | tf_op jit(solution)/shard_map/transpose(jvp())/while
  406.6 4.7 %copy-start.41 = (f32[10]{0:T(128)}, f32[10]{0:T(128)S(1)}, u32[]{:S(2)}) copy-start(f32[10]{0:T(128)S(1)} %get-tuple-element.870) | copy-start | bytes 124 | tf_op jit(solution)/shard_map/transpose(jvp())/while
  414.5 4.2 copy-start.4
  424.8 4.9 %copy-start.42 = (f32[10]{0:T(128)S(1)}, f32[10]{0:T(128)}, u32[]{:S(2)}) copy-start(f32[10]{0:T(128)} %copy-done.41) | copy-start | bytes 124 | tf_op jit(solution)/shard_map/transpose(jvp())/while
  429.6 4.7 %copy-start.41 = (f32[10]{0:T(128)}, f32[10]{0:T(128)S(1)}, u32[]{:S(2)}) copy-start(f32[10]{0:T(128)S(1)} %get-tuple-element.870) | copy-start | bytes 124 | tf_op jit(solution)/shard_map/transpose(jvp())/while
  437.5 4.2 copy-start.4
  447.8 4.9 %copy-start.42 = (f32[10]{0:T(128)S(1)}, f32[10]{0:T(128)}, u32[]{:S(2)}) copy-start(f32[10]{0:T(128)} %copy-done.41) | copy-start | bytes 124 | tf_op jit(solution)/shard_map/transpose(jvp())/while
  455.6 1.6 copy-start.12
  455.6 1.6 copy-start.35
  455.6 1.6 copy-start.37
Sparse Core Ops, SparseCore 0:
  94.4 43.0 all-gather.16
  139.3 47.8 all-gather.18
  189.0 24.9 all-gather.12
  251.5 70.5 all-gather.20
  324.9 44.7 all-gather.14
where the time goes:
time: 470 us; the launch traced here: 465 us
  waiting for transfers between devices  135 us (29%)
  local copies, waits for them, and re-layouts  103 us (22%)
  matrix products  73.2 us (16%)
  other arithmetic  58.5 us (12%)
  blocking collectives  56 us (12%)
  between operations  15.2 us (3%)
  starting transfers between devices  13.3 us (3%)
  loops' own time  9.53 us (2%)
    all_gather x4, waiting for transfers between devices, carried_in(): pieces = jax.tree.map(lambda part: lax.all_gather(part, axis), running)  84.6 us
    dynamic_update_slice x6, local copies, waits for them, and re-layouts, ssd_local(): lax.scan(stepper, state_in, (x_blocks, dt_blocks, b_blocks, c_blocks))  47.3 us
    dot_general x9, matrix products, group_step(): jnp.einsum('hts,shp->thp', decay_mat * affinity[None], weighted, precisio...  38.2 us
    all_gather x1, waiting for transfers between devices, gather_in_order(): parts = lax.all_gather(parts, axes[k])  29.1 us
    another operation x33, other arithmetic  22.9 us
    unnamed x1, blocking collectives  17.2 us
    all_to_all x1, waiting for transfers between devices, sum_at_owner(): lax.all_to_all(parts, axis, split_axis=0, concat_axis=0, tiled=True)  16.9 us
    all_gather x2, blocking collectives, carried_in(): pieces = jax.tree.map(lambda part: lax.all_gather(part, axis), running)  15.8 us
  transfers between devices with their start and end apart: 7, of which 7 were waited for; matrix products, arithmetic and copies ran while one was open for 11% of the time, Pallas kernels for 0%

commit v1 on v0

v1 whole, which is shorter than its diff:
```python
import functools

import jax
import jax.numpy as jnp
from jax import lax
from jax.experimental import pallas as pl
from jax.experimental.pallas import tpu as pltpu
from jax.sharding import Mesh
from jax.sharding import PartitionSpec as P

SEQ = ("seq_0", "seq_1")
Q = 128
HEAD = 64
EPS = 1e-05
F32 = jnp.float32
BF16 = jnp.bfloat16
HI = lax.Precision.HIGHEST
NN = (((1,), (0,)), ((), ()))
NT = (((1,), (1,)), ((), ()))


def mm(a, b, dims=NN):
    return lax.dot_general(a, b, dims, preferred_element_type=F32)


def mm_exact(a, b, dims=NN):
    return lax.dot_general(a, b, dims, precision=HI, preferred_element_type=F32)


def split_mm(a, b, dims):
    high = b.astype(BF16)
    low = (b - high.astype(F32)).astype(BF16)
    return mm(a, high, dims) + mm(a, low, dims)


def iota(shape, dim):
    return lax.broadcasted_iota(jnp.int32, shape, dim)


def head_sum_matrix(width):
    return (iota((16, width), 1) // HEAD == iota((16, width), 0)).astype(BF16)


def log_decays(dt, a_log):
    return -jnp.exp(a_log) * dt


def run_rows(la):
    upper = (iota((Q, Q), 0) <= iota((Q, Q), 1)).astype(F32)
    return mm_exact(la, upper)


def run_cols(la):
    lower = (iota((Q, Q), 0) >= iota((Q, Q), 1)).astype(F32)
    return mm_exact(lower, la, NT)


def pair_row(column, j):
    lane = iota((1, 2 * HEAD), 1)
    return jnp.where(lane < HEAD, column[2 * j : 2 * j + 1, :], column[2 * j + 1 : 2 * j + 2, :])


def halves(pair):
    lane = iota(pair.shape, 1)
    zero = jnp.zeros_like(pair)
    return (jnp.where(lane < HEAD, pair, zero), jnp.where(lane >= HEAD, pair, zero))


def pair_slice(j):
    return slice(2 * HEAD * j, 2 * HEAD * (j + 1))


def sigmoid(v):
    return 1.0 / (1.0 + jnp.exp(-v))


def outer_state(left_t, weights, right, j):
    lhs = jnp.concatenate(
        [(left_t * weights[h : h + 1, :]).astype(BF16) for h in (2 * j, 2 * j + 1)], axis=1
    )
    first, second = halves(right)
    return mm(lhs, jnp.concatenate([first, second], axis=0).astype(BF16))


def state_kernel(dt_ref, alog_ref, x_ref, b_ref, inc_ref, state_ref, ldev_ref):
    @pl.when(pl.program_id(0) == 0)
    def _():
        state_ref[...] = jnp.zeros_like(state_ref)
        ldev_ref[...] = jnp.zeros_like(ldev_ref)

    dt = dt_ref[...]
    run = run_rows(log_decays(dt, alog_ref[...]))
    total = run[:, Q - 1 :]
    weights = jnp.exp(total - run) * dt
    b_t = jnp.transpose(b_ref[...].astype(F32))
    for j in range(dt.shape[0] // 2):
        cols = pair_slice(j)
        inc = outer_state(b_t, weights, x_ref[:, cols].astype(F32), j)
        inc_ref[0, :, cols] = inc
        row = pair_row(total, j)
        state_ref[:, cols] = jnp.exp(row) * state_ref[:, cols] + inc
        ldev_ref[:, cols] += row


def y_kernel(
    dt_ref, alog_ref, x_ref, b_ref, c_ref, inc_ref, in_ref, z_ref, skip_ref,
    y_ref, end_ref, sq_ref, state,
):
    @pl.when(pl.program_id(0) == 0)
    def _():
        state[...] = in_ref[...]

    dt = dt_ref[...]
    la = log_decays(dt, alog_ref[...])
    run, cols_run = run_rows(la), run_cols(la)
    total = run[:, Q - 1 :]
    c_part = c_ref[...]
    c_vals = c_part.astype(F32)
    affinity = mm(c_part, b_ref[...], NT)
    causal = iota((Q, Q), 0) >= iota((Q, Q), 1)
    squares = jnp.zeros((Q, 2 * HEAD), F32)
    for j in range(dt.shape[0] // 2):
        cols = pair_slice(j)
        x_pair = x_ref[:, cols]
        x_first, x_second = halves(x_pair.astype(F32))
        before = state[:, cols]
        s_first, s_second = halves(before)
        left = []
        for h in (2 * j, 2 * j + 1):
            at = jnp.broadcast_to(cols_run[:, h : h + 1], (Q, Q))
            decay = jnp.exp(jnp.where(causal, at - run[h : h + 1, :], -1e30))
            left.append((decay * affinity * dt[h : h + 1, :]).astype(BF16))
            left.append((jnp.exp(at[:, : c_vals.shape[1]]) * c_vals).astype(BF16))
        lhs = jnp.concatenate(left, axis=1)
        rhs = jnp.concatenate([x_first, s_first, x_second, s_second], axis=0).astype(BF16)
        y_pair = mm(lhs, rhs)
        y_ref[:, cols] = y_pair
        after = jnp.exp(pair_row(total, j)) * before + inc_ref[0, :, cols]
        end_ref[0, :, cols] = after
        state[:, cols] = after
        z = z_ref[:, cols].astype(F32)
        gated = (y_pair + skip_ref[:, cols] * x_pair.astype(F32)) * (z * sigmoid(z))
        squares += gated * gated
    sq_ref[...] = split_mm(jnp.ones((8, 2 * HEAD), BF16), squares, NT)[:1]


def token_column(row):
    eye = (iota((Q, Q), 0) == iota((Q, Q), 1)).astype(F32)
    return mm_exact(eye, jnp.broadcast_to(row, (8, Q)), NT)[:, :1]


def gate_kernel(
    full_width,
    dt_ref, alog_ref, c_ref, y_ref, x_ref, z_ref, g_ref, skip_ref, gain_ref, sq_ref, dot_ref,
    gy_ref, dz_ref, inc_ref, state_ref,
):
    @pl.when(pl.program_id(0) == 0)
    def _():
        state_ref[...] = jnp.zeros_like(state_ref)

    dt = dt_ref[...]
    run = run_rows(log_decays(dt, alog_ref[...]))
    total = run[:, Q - 1 :]
    grow = jnp.exp(run)
    c_t = jnp.transpose(c_ref[...].astype(F32))
    inverse = lax.rsqrt(sq_ref[...] / full_width + EPS)
    inv_col = token_column(inverse)
    dot_col = token_column(inverse * inverse * inverse * dot_ref[...] / full_width)
    for j in range(dt.shape[0] // 2):
        cols = pair_slice(j)
        z = z_ref[:, cols].astype(F32)
        sig = sigmoid(z)
        act = z * sig
        y = y_ref[:, cols] + skip_ref[:, cols] * x_ref[:, cols].astype(F32)
        scaled = g_ref[:, cols].astype(F32) * gain_ref[:, cols]
        grad_gated = inv_col * scaled - (y * act) * dot_col
        dz_ref[:, cols] = (grad_gated * y * sig * (1.0 + z * (1.0 - sig))).astype(BF16)
        gy = (grad_gated * act).astype(BF16)
        gy_ref[:, cols] = gy
        inc = outer_state(c_t, grow, gy.astype(F32), j)
        inc_ref[0, :, cols] = inc
        state_ref[:, cols] = jnp.exp(pair_row(total, j)) * state_ref[:, cols] + inc


def grad_kernel(
    dt_ref, alog_ref, x_ref, b_ref, c_ref, y_ref, gy_ref, inc_ref, end_ref, in_ref, skip_ref,
    dx_ref, ddt_ref, state, prod,
):
    @pl.when(pl.program_id(0) == 0)
    def _():
        state[...] = in_ref[...]

    dt = dt_ref[...]
    heads = dt.shape[0]
    width = heads * HEAD
    a_log = alog_ref[...]
    la = log_decays(dt, a_log)
    run, cols_run = run_rows(la), run_cols(la)
    total = run[:, Q - 1 :]
    eye = (iota((Q, Q), 0) == iota((Q, Q), 1)).astype(F32)
    cols_dt = mm_exact(eye, dt, NT)
    b_part = b_ref[...]
    b_vals = b_part.astype(F32)
    affinity = mm(b_part, c_ref[...], NT)
    later = iota((Q, Q), 1) >= iota((Q, Q), 0)
    lane = iota((Q, 2 * HEAD), 1)
    for j in range(heads // 2):
        cols = pair_slice(j)
        gy = gy_ref[:, cols].astype(F32)
        g_first, g_second = halves(gy)
        after = state[:, cols]
        s_first, s_second = halves(after)
        left = []
        for h in (2 * j, 2 * j + 1):
            at = jnp.broadcast_to(cols_run[:, h : h + 1], (Q, Q))
            decay = jnp.exp(jnp.where(later, run[h : h + 1, :] - at, -1e30))
            left.append((decay * affinity).astype(BF16))
            tail = total[h : h + 1, :] - at[:, : b_vals.shape[1]]
            left.append((jnp.exp(tail) * b_vals).astype(BF16))
        lhs = jnp.concatenate(left, axis=1)
        rhs = jnp.concatenate([g_first, s_first, g_second, s_second], axis=0).astype(BF16)
        grad_in = mm(lhs, rhs)
        step = jnp.where(
            lane < HEAD, cols_dt[:, 2 * j : 2 * j + 1], cols_dt[:, 2 * j + 1 : 2 * j + 2]
        )
        scaled = step * grad_in
        dx_ref[:, cols] = (scaled + skip_ref[:, cols] * gy).astype(BF16)
        x = x_ref[:, cols].astype(F32)
        prod[0, :, cols] = x * grad_in
        prod[1, :, cols] = gy * y_ref[:, cols] - x * scaled
        crossing = (after * end_ref[0, :, cols]).reshape(-1, 8, 2 * HEAD)
        prod[2, :8, cols] = jnp.sum(crossing, axis=0)
        state[:, cols] = jnp.exp(pair_row(total, j)) * after + inc_ref[0, :, cols]
    heads_of = head_sum_matrix(width)
    direct = split_mm(heads_of, prod[0], NT)[:heads]
    change = split_mm(heads_of, prod[1], NT)[:heads]
    cross = jnp.sum(split_mm(heads_of, prod[2, :8, :], NT), axis=1, keepdims=True)[:heads]
    lower = (iota((Q, Q), 0) >= iota((Q, Q), 1)).astype(F32)
    grad_la = mm_exact(change, lower) + cross
    ddt_ref[...] = direct - jnp.exp(a_log) * grad_la


def scan_kernel(pair_in, reverse, in_ref, decay_ref, out_ref):
    peers = in_ref.shape[0]
    low = iota((8, in_ref.shape[2]), 0) < 4
    running = jnp.zeros(in_ref.shape[1:], F32)
    for k in reversed(range(peers)) if reverse else range(peers):
        high = running.astype(BF16).astype(F32)
        rest = pltpu.roll(running - high, 4, 0)
        out_ref[k] = jnp.where(low, high, rest).astype(BF16)
        part = in_ref[k].astype(F32)
        if pair_in:
            part = part + pltpu.roll(part, 4, 0)
        running = decay_ref[k] * running + part


def call(kernel, grid, in_specs, out_specs, out_shape, scratch=(), flops=2e9, name=None):
    return pl.pallas_call(
        kernel,
        grid=grid,
        in_specs=in_specs,
        out_specs=out_specs,
        out_shape=out_shape,
        scratch_shapes=scratch,
        name=name,
        compiler_params=pltpu.CompilerParams(
            dimension_semantics=("arbitrary",) * len(grid), vmem_limit_bytes=40 << 20
        ),
        cost_estimate=pl.CostEstimate(
            flops=int(flops), bytes_accessed=8 << 20, transcendentals=0
        ),
    )


def spread(state):
    peers = lax.axis_size(SEQ[0]) * lax.axis_size(SEQ[1])
    return state.reshape(peers, -1, state.shape[1])


def shards(
    x_in, z_gate, b_proj, c_proj, dt_step, a_log, skip_gain, norm_gain, out_weight, out_grad
):
    length, width = x_in.shape
    heads = a_log.shape[0]
    blocks = length // Q
    nstate = b_proj.shape[1]
    full_width = width * lax.axis_size("chan")
    alog = a_log[:, None]
    skip_row = jnp.repeat(skip_gain, HEAD)[None]
    gain_row = norm_gain[None]

    def shape(*dims, kind=F32):
        return jax.ShapeDtypeStruct(dims, kind)

    def specs(order):
        return dict(
            dt=pl.BlockSpec((heads, Q), lambda i: (0, order(i))),
            alog=pl.BlockSpec((heads, 1), lambda i: (0, 0)),
            wide=pl.BlockSpec((Q, width), lambda i: (order(i), 0)),
            bc=pl.BlockSpec((Q, nstate), lambda i: (order(i), 0)),
            inc=pl.BlockSpec((1, nstate, width), lambda i: (order(i), 0, 0)),
            state=pl.BlockSpec((nstate, width), lambda i: (0, 0)),
            row=pl.BlockSpec((1, width), lambda i: (0, 0)),
            tok=pl.BlockSpec((1, Q), lambda i: (0, order(i))),
        )

    up = specs(lambda i: i)
    down = specs(lambda i: blocks - 1 - i)

    inc, own_state, log_device = call(
        state_kernel,
        (blocks,),
        [up["dt"], up["alog"], up["wide"], up["bc"]],
        [up["inc"], up["state"], up["row"]],
        [shape(blocks, nstate, width), shape(nstate, width), shape(1, width)],
        name="own_state",
    )(dt_step, alog, x_in, b_proj)

    parts = spread(own_state)
    peers = parts.shape[0]
    d1 = log_device.astype(BF16)
    d2 = (log_device - d1.astype(F32)).astype(BF16)
    d3 = (log_device - d1.astype(F32) - d2.astype(F32)).astype(BF16)
    logs = jnp.concatenate([d1, d2, d3, jnp.zeros_like(d1)], axis=0)
    payload = jnp.concatenate(
        [parts.astype(BF16), jnp.broadcast_to(logs[None], (peers, 4, width))], axis=1
    )
    arrived = lax.all_to_all(payload, SEQ, 0, 0, tiled=True)
    decays = jnp.exp(jnp.sum(arrived[:, 4:7].astype(F32), axis=1, keepdims=True))

    def scanned(arrived, pair_in, reverse, name):
        whole = pl.BlockSpec((peers, 8, width), lambda i: (0, 0, 0))
        return call(
            functools.partial(scan_kernel, pair_in, reverse),
            (1,),
            [whole, pl.BlockSpec((peers, 1, width), lambda i: (0, 0, 0))],
            whole,
            shape(peers, 8, width, kind=BF16),
            name=name,
        )(arrived, decays)

    def entering(scanned_parts):
        back = lax.all_to_all(scanned_parts, SEQ, 0, 0, tiled=True).astype(F32)
        return (back[:, :4] + back[:, 4:]).reshape(nstate, width)

    state_in = entering(scanned(arrived, False, False, "scan_up"))

    y, ends, squares = call(
        y_kernel,
        (blocks,),
        [up["dt"], up["alog"], up["wide"], up["bc"], up["bc"], up["inc"], up["state"],
         up["wide"], up["row"]],
        [up["wide"], up["inc"], up["tok"]],
        [shape(length, width), shape(blocks, nstate, width), shape(1, length)],
        [pltpu.VMEM((nstate, width), F32)],
        name="y",
    )(dt_step, alog, x_in, b_proj, c_proj, inc, state_in, z_gate, skip_row)

    def chan_sum(value):
        size = lax.axis_size("chan")
        copies = jnp.broadcast_to(value[None], (size, *value.shape))
        return jnp.sum(lax.all_to_all(copies, "chan", 0, 0, tiled=True), axis=0)

    square_sum = chan_sum(squares)
    z_vals = z_gate.astype(F32)
    gated = (y + skip_row * x_in.astype(F32)) * (z_vals * sigmoid(z_vals))
    inverse = lax.rsqrt(square_sum[0] / full_width + EPS)
    normed = (gated * inverse[:, None] * gain_row).astype(BF16)
    partial = lax.dot_general(
        out_grad, normed, (((0,), (0,)), ((), ())), preferred_element_type=F32
    ).astype(BF16)

    weight = out_weight
    for axis in SEQ:
        weight = lax.all_gather(weight, axis)
    weight = jnp.swapaxes(weight, 0, 1).reshape(-1, width)
    grad_norm = mm(out_grad, weight).astype(BF16)
    dots = jnp.sum(gated * (grad_norm.astype(F32) * gain_row), axis=1)[None]
    dot_sum = chan_sum(dots)

    x_peers, z_peers = lax.axis_size(SEQ[0]), lax.axis_size(SEQ[1])
    held = partial.reshape(x_peers, -1, width)
    held = lax.all_to_all(held, SEQ[0], 0, 0, tiled=True).astype(F32).sum(0).astype(BF16)
    held = held.reshape(z_peers, -1, width)
    weight_grad = lax.all_to_all(held, SEQ[1], 0, 0, tiled=True).astype(F32).sum(0)

    grad_y, grad_z, grad_inc, own_grad = call(
        functools.partial(gate_kernel, float(full_width)),
        (blocks,),
        [down["dt"], down["alog"], down["bc"], down["wide"], down["wide"], down["wide"],
         down["wide"], down["row"], down["row"], down["tok"], down["tok"]],
        [down["wide"], down["wide"], down["inc"], down["state"]],
        [shape(length, width, kind=BF16), shape(length, width, kind=BF16),
         shape(blocks, nstate, width), shape(nstate, width)],
        name="gate",
    )(dt_step, alog, c_proj, y, x_in, z_gate, grad_norm, skip_row, gain_row, square_sum, dot_sum)

    parts = spread(own_grad)
    high = parts.astype(BF16)
    payload = jnp.concatenate([high, (parts - high.astype(F32)).astype(BF16)], axis=1)
    arrived = lax.all_to_all(payload, SEQ, 0, 0, tiled=True)
    grad_out = entering(scanned(arrived, True, True, "scan_down"))

    grad_x, grad_dt = call(
        grad_kernel,
        (blocks,),
        [down["dt"], down["alog"], down["wide"], down["bc"], down["bc"], down["wide"],
         down["wide"], down["inc"], down["inc"], down["state"], down["row"]],
        [down["wide"], down["dt"]],
        [shape(length, width, kind=BF16), shape(heads, length)],
        [pltpu.VMEM((nstate, width), F32), pltpu.VMEM((3, Q, width), F32)],
        name="grad",
    )(dt_step, alog, x_in, b_proj, c_proj, y, grad_y, grad_inc, ends, grad_out, skip_row)
    return (grad_x, grad_z, grad_dt, weight_grad)


def solution(mesh):
    z_axis = 8 if mesh.shape["seq"] % 8 == 0 else 2
    torus = Mesh(
        mesh.devices.reshape(-1, z_axis, mesh.shape["chan"]), ("seq_0", "seq_1", "chan")
    )
    return jax.shard_map(
        shards,
        mesh=torus,
        in_specs=(
            P(SEQ, "chan"),
            P(SEQ, "chan"),
            P(SEQ, None),
            P(SEQ, None),
            P("chan", SEQ),
            P("chan"),
            P("chan"),
            P("chan"),
            P(SEQ, "chan"),
            P(SEQ, None),
        ),
        out_specs=(P(SEQ, "chan"), P(SEQ, "chan"), P("chan", SEQ), P(SEQ, "chan")),
        check_vma=False,
    )
```

time: 470 us -> 253 us (0.54)
  waiting for transfers between devices: 135 us -> 68.7 us
  matrix products: 73.2 us -> 9.98 us
  local copies, waits for them, and re-layouts: 103 us -> 40.2 us
  other arithmetic: 58.5 us -> 9.81 us
  starting transfers between devices: 13.3 us -> 43.7 us
  Pallas kernels: 0 us -> 26 us
  blocking collectives: 56 us -> 35.3 us
  loops' own time: 9.53 us -> 0 us
    all_gather x5 -> x1, waiting for transfers between devices: 114 us -> 0.02 us  [shards(): weight = lax.all_gather(weight, axis)]
    dot_general x34 -> x2, matrix products: 73.2 us -> 9.98 us  [the longest x1 5.46 us: shards(): lax.dot_general(out_grad, normed, (((0,), (0,)), ((), ())), preferred_ele...]
    dynamic_update_slice x6 -> x0, local copies, waits for them, and re-layouts: 47.3 us -> none  [ssd_local(): lax.scan(stepper, state_in, (x_blocks, dt_blocks, b_blocks, c_blocks))]
    all_to_all x2 -> x7, waiting for transfers between devices: 21.6 us -> 68.6 us  [the longest x1 20.5 us: shards(): lax.all_to_all(held, SEQ[1], 0, 0, tiled=True).astype(F32).sum(0)]
    all_to_all x2 -> x7, starting transfers between devices: 13.2 us -> 43.6 us  [the longest x2 15.3 us: chan_sum(): return jnp.sum(lax.all_to_all(copies, 'chan', 0, 0, tiled=True), axis=0)]
    pallas_call x0 -> x6, Pallas kernels: none -> 26 us  [the longest x1 9.34 us: shards(): call(grad_kernel, (blocks,), [down['dt'], down['alog'], down['wide'], dow...]
    another operation x33 -> x0, other arithmetic: 22.9 us -> none
    unnamed x1 -> x0, blocking collectives: 17.2 us -> none
  transfers between devices with their start and end apart: 7 -> 8, of which waited for: 7 -> 6; matrix products, arithmetic and copies ran while one was open for 11% -> 10% of each run, Pallas kernels for 0% -> 7%
where the time goes in v1:
time: 253 us; the launch traced here: 248 us
  waiting for transfers between devices  68.7 us (27%)
  starting transfers between devices  43.7 us (17%)
  local copies, waits for them, and re-layouts  40.2 us (16%)
  blocking collectives  35.3 us (14%)
  Pallas kernels  26 us (10%)
  between operations  14.4 us (6%)
  matrix products  9.98 us (4%)
  other arithmetic  9.81 us (4%)
    unnamed x76, local copies, waits for them, and re-layouts  26.8 us
    all_to_all x1, blocking collectives, shards(): arrived = lax.all_to_all(payload, SEQ, 0, 0, tiled=True)  22.4 us
    all_to_all x1, waiting for transfers between devices, shards(): lax.all_to_all(held, SEQ[1], 0, 0, tiled=True).astype(F32).sum(0)  20.5 us
    all_to_all x2, waiting for transfers between devices, entering(): back = lax.all_to_all(scanned_parts, SEQ, 0, 0, tiled=True).astype(F32)  20 us
    all_to_all x1, waiting for transfers between devices, shards(): lax.all_to_all(held, SEQ[0], 0, 0, tiled=True).astype(F32).sum(0)  20 us
    all_to_all x2, starting transfers between devices, chan_sum(): return jnp.sum(lax.all_to_all(copies, 'chan', 0, 0, tiled=True), axis=0)  15.3 us
    all_to_all x2, starting transfers between devices, entering(): back = lax.all_to_all(scanned_parts, SEQ, 0, 0, tiled=True).astype(F32)  13.1 us
    all_gather x1, blocking collectives, shards(): weight = lax.all_gather(weight, axis)  12.9 us
  transfers between devices with their start and end apart: 8, of which 6 were waited for; matrix products, arithmetic and copies ran while one was open for 10% of the time, Pallas kernels for 7%

profile of v1, /device:TPU:1, one launch (start us, length us, event | category | flops | bytes accessed | tf_op | source)
XLA Modules:
  0.0 248.1 jit_solution(14473353192062869669)
XLA Ops:
  7.2 12.9 %all-gather = bf16[320,640]{1,0:T(8,128)(2,1)} all-gather(bf16[80,640]{1,0:T(8,128)(2,1)} %param.18), channel_id=2, replica_groups=mesh['seq_0'=4,'seq_1'=8,'chan'=8] {'seq_0'}, dimensions={0}, use_global_device_ids=true | all-gather | bytes 512000 | tf_op jit(solution)/shard_map/all_gather | solution.py:375
  20.1 0.7 copy.63.alog_ref
  20.9 1.2 copy-done.4
  22.1 0.9 copy-done.9
  23.0 0.8 copy-done.14
  23.8 4.0 %own_state.1 = (f32[6,128,640]{2,1,0:T(8,128)S(1)}, f32[128,640]{1,0:T(8,128)S(1)}, f32[1,640]{1,0:T(1,128)S(1)}) custom-call(f32[10,768]{1,0:T(8,128)S(1)} %copy-done.14, f32[10,1]{1,0:T(8,128)S(1)} %copy.63.alog_ref, bf16[768,640]{1,0:T(8,128)(2,1)S(1)} %copy-done.4, bf16[768,128]{1,0:T(8,128)(2,1)S(1)} %copy-done.9), custom_call_target="tpu_custom_call" | custom-call | flops 2000000000 | bytes 8388608 | tf_op jit(solution)/shard_map/own_state/pallas_call | solution.py:310
  28.3 22.4 %all_to_all.40.in_ref = bf16[32,8,640]{2,1,0:T(8,128)(2,1)S(1)} all-to-all(bf16[32,8,640]{2,1,0:T(8,128)(2,1)S(1)} %pad_maximum_fusion), channel_id=1, replica_groups=mesh['seq_0'=4,'seq_1'=8,'chan'=8] {'seq_0','seq_1'}, dimensions={0} | all-to-all | bytes 655360 | tf_op jit(solution)/shard_map/all_to_all | solution.py:328
  51.0 0.9 scan_up.1
  51.9 7.2 %all-to-all-start.1 = ((bf16[32,8,640]{2,1,0:T(8,128)(2,1)}), bf16[32,8,640]{2,1,0:T(8,128)(2,1)S(1)}, u32[]{:S(2)}, u32[]{:S(2)}) async-start(bf16[32,8,640]{2,1,0:T(8,128)(2,1)} %scan_up.1), calls=%async_computation.1 | async-start | bytes 655360 | tf_op jit(solution)/shard_map/all_to_all | solution.py:343
  59.2 0.6 broadcast_in_dim_reshape.3.skip_ref
  59.8 12.0 %all-to-all-done.1 = bf16[32,8,640]{2,1,0:T(8,128)(2,1)S(1)} async-done(((bf16[32,8,640]{2,1,0:T(8,128)(2,1)}), bf16[32,8,640]{2,1,0:T(8,128)(2,1)S(1)}, u32[]{:S(2)}, u32[]{:S(2)}) %all-to-all-start.1) | async-done | bytes 327712 | tf_op jit(solution)/shard_map/all_to_all | solution.py:343
  72.1 0.9 copy-done.11
  73.1 0.8 copy-done.15
  73.9 0.7 copy-done.19
  74.6 0.7 copy-done.22
  75.2 1.2 copy-done.28
  76.4 1.5 copy-done.32
  78.0 5.8 %y.1 = (f32[768,640]{1,0:T(8,128)S(1)}, f32[6,128,640]{2,1,0:T(8,128)S(1)}, f32[1,768]{1,0:T(1,128)S(1)}) custom-call(f32[10,768]{1,0:T(8,128)S(1)} %copy-done.15, f32[10,1]{1,0:T(8,128)S(1)} %copy-done.19, bf16[768,640]{1,0:T(8,128)(2,1)S(1)} %copy-done.5, bf16[768,128]{1,0:T(8,128)(2,1)S(1)} %copy-done.10, bf16[768,128]{1,0:T(8,128)(2,1)S(1)} %copy-done.11, ...), custom_call_target="tpu_custom_call" | custom-call | flops 2000000000 | bytes 8388608 | tf_op jit(solution)/shard_map/y/pallas_call | solution.py:348
  83.7 1.4 copy-done
  85.7 0.7 reduce.3
  86.4 0.6 broadcast_in_dim.39
  87.0 11.3 %all-to-all-start.2 = ((f32[8,1,768]{2,1,0:T(1,128)}), f32[8,1,768]{2,1,0:T(1,128)S(1)}, u32[]{:S(2)}, u32[]{:S(2)}) async-start(f32[8,1,768]{2,1,0:T(1,128)} %broadcast_in_dim.39), calls=%async_computation.2 | async-start | bytes 49152 | tf_op jit(solution)/shard_map/all_to_all | solution.py:362
  98.3 0.8 mul.41
  99.1 3.9 %all-to-all-done.2 = f32[8,1,768]{2,1,0:T(1,128)S(1)} async-done(((f32[8,1,768]{2,1,0:T(1,128)}), f32[8,1,768]{2,1,0:T(1,128)S(1)}, u32[]{:S(2)}, u32[]{:S(2)}) %all-to-all-start.2) | async-done | bytes 24608 | tf_op jit(solution)/shard_map/all_to_all | solution.py:362
  103.1 2.4 copy.58
  105.5 1.0 copy-done.37
  106.5 4.5 %multiply_reduce_fusion = (f32[768]{0:T(1024)S(1)}, bf16[768,640]{1,0:T(8,128)(2,1)}) fusion(f32[640]{0:T(1024)S(1)} %copy-done.35, bf16[768,640]{1,0:T(8,128)(2,1)S(1)} %copy-done.29, f32[768,640]{1,0:T(8,128)S(1)} %get-tuple-element.19.y_ref, bf16[768,640]{1,0:T(8,128)(2,1)S(1)} %copy-done.5, f32[640]{0:T(1024)S(1)} %mul.41, ...), kind=kOutput, calls=%fused_computation.9 | convolution fusion | flops 2523462912 | bytes 12132352 | tf_op jit(solution)/shard_map/dot_general | solution.py:23
  111.0 0.6 broadcast_in_dim.40
  111.6 4.0 %all-to-all-start.3 = ((f32[8,1,768]{2,1,0:T(1,128)}), f32[8,1,768]{2,1,0:T(1,128)S(1)}, u32[]{:S(2)}, u32[]{:S(2)}) async-start(f32[8,1,768]{2,1,0:T(1,128)} %broadcast_in_dim.40), calls=%async_computation.3 | async-start | bytes 49152 | tf_op jit(solution)/shard_map/all_to_all | solution.py:362
  115.6 5.5 %convolution_convert_fusion = bf16[640,2560]{1,0:T(8,128)(2,1)S(1)} fusion(bf16[768,2560]{1,0:T(8,128)(2,1)} %param.19, f32[768]{0:T(1024)S(1)} %add_rsqrt_fusion, f32[640]{0:T(1024)S(1)} %copy-done.35, bf16[768,640]{1,0:T(8,128)(2,1)} %z_ref.3, f32[768,640]{1,0:T(8,128)S(1)} %get-tuple-element.19.y_ref, bf16[768,640]{1,0:T(8,128)(2,1)S(1)} %copy-done.5, ...), kind=kOutput, calls=%fused_computation | convolution fusion | flops 2524119040 | bytes 11149312 | tf_op jit(solution)/shard_map/dot_general | solution.py:369
  121.1 2.0 copy.73
  123.1 4.7 %all-to-all-start.6 = ((bf16[4,640,640]{1,2,0:T(8,128)(2,1)}), bf16[4,640,640]{1,2,0:T(8,128)(2,1)}, u32[]{:S(2)}, u32[]{:S(2)}) async-start(bf16[4,640,640]{1,2,0:T(8,128)(2,1)} %bitcast.16), calls=%async_computation.6 | async-start | bytes 6553600 | tf_op jit(solution)/shard_map/all_to_all | solution.py:383
  129.0 0.9 copy-done.12
  129.9 0.8 copy-done.16
  130.7 0.7 copy-done.20
  131.4 0.7 copy-done.23
  132.0 0.7 copy-done.25
  132.7 0.7 copy-done.27
  133.4 1.2 copy-done.30
  134.6 1.2 copy-done.33
  135.8 5.8 %gate.1 = (bf16[768,640]{1,0:T(8,128)(2,1)S(1)}, bf16[768,640]{1,0:T(8,128)(2,1)}, f32[6,128,640]{2,1,0:T(8,128)S(1)}, f32[128,640]{1,0:T(8,128)S(1)}) custom-call(f32[10,768]{1,0:T(8,128)S(1)} %copy-done.16, f32[10,1]{1,0:T(8,128)S(1)} %copy-done.20, bf16[768,128]{1,0:T(8,128)(2,1)S(1)} %copy-done.12, f32[768,640]{1,0:T(8,128)S(1)} %get-tuple-element.19.y_ref, ...), custom_call_target="tpu_custom_call" | custom-call | flops 2000000000 | bytes 8388608 | tf_op jit(solution)/shard_map/gate/pallas_call | solution.py:387
  141.6 1.3 copy-done.2
  142.9 0.9 copy-done.6
  143.9 0.8 reshape.56
  144.7 1.2 subtract_convert_fusion
  145.9 0.9 pad_maximum_fusion.1
  146.8 20.0 %all-to-all-done.6 = bf16[4,640,640]{1,2,0:T(8,128)(2,1)} async-done(((bf16[4,640,640]{1,2,0:T(8,128)(2,1)}), bf16[4,640,640]{1,2,0:T(8,128)(2,1)}, u32[]{:S(2)}, u32[]{:S(2)}) %all-to-all-start.6) | async-done | bytes 3276832 | tf_op jit(solution)/shard_map/all_to_all | solution.py:383
  166.8 5.3 %all-to-all-start.4 = ((bf16[32,8,640]{2,1,0:T(8,128)(2,1)}), bf16[32,8,640]{2,1,0:T(8,128)(2,1)S(1)}, u32[]{:S(2)}, u32[]{:S(2)}) async-start(bf16[32,8,640]{2,1,0:T(8,128)(2,1)} %pad_maximum_fusion.1), calls=%async_computation.4 | async-start | bytes 655360 | tf_op jit(solution)/shard_map/all_to_all | solution.py:401
  172.1 3.5 %reduce_sum.67 = bf16[640,640]{0,1:T(8,128)(2,1)} reduce(bf16[4,640,640]{1,2,0:T(8,128)(2,1)} %all-to-all-done.6, bf16[]{:T(256)} %constant.2.clone.1), dimensions={0}, to_apply=%region_4.0 | reduce | flops 1228800 | bytes 4096002 | tf_op jit(solution)/shard_map/reduce_sum | solution.py:383
  175.6 2.2 copy.66
  177.8 4.3 %all-to-all-done.4.in_ref = bf16[32,8,640]{2,1,0:T(8,128)(2,1)S(1)} async-done(((bf16[32,8,640]{2,1,0:T(8,128)(2,1)}), bf16[32,8,640]{2,1,0:T(8,128)(2,1)S(1)}, u32[]{:S(2)}, u32[]{:S(2)}) %all-to-all-start.4) | async-done | bytes 327712 | tf_op jit(solution)/shard_map/all_to_all | solution.py:401
  182.1 5.3 %all-to-all-start.7 = ((bf16[8,80,640]{2,1,0:T(8,128)(2,1)}), bf16[8,80,640]{2,1,0:T(8,128)(2,1)}, u32[]{:S(2)}, u32[]{:S(2)}) async-start(bf16[8,80,640]{2,1,0:T(8,128)(2,1)} %bitcast.20), calls=%async_computation.7 | async-start | bytes 1638400 | tf_op jit(solution)/shard_map/all_to_all | solution.py:385
  187.6 0.7 copy-done.8
  188.3 20.5 %all-to-all-done.7 = bf16[8,80,640]{2,1,0:T(8,128)(2,1)} async-done(((bf16[8,80,640]{2,1,0:T(8,128)(2,1)}), bf16[8,80,640]{2,1,0:T(8,128)(2,1)}, u32[]{:S(2)}, u32[]{:S(2)}) %all-to-all-start.7) | async-done | bytes 819232 | tf_op jit(solution)/shard_map/all_to_all | solution.py:385
  208.8 5.9 %all-to-all-start.5 = ((bf16[32,8,640]{2,1,0:T(8,128)(2,1)}), bf16[32,8,640]{2,1,0:T(8,128)(2,1)S(1)}, u32[]{:S(2)}, u32[]{:S(2)}) async-start(bf16[32,8,640]{2,1,0:T(8,128)(2,1)} %copy-done.8), calls=%async_computation.5 | async-start | bytes 655360 | tf_op jit(solution)/shard_map/all_to_all | solution.py:343
  214.8 2.0 convert_reduce_fusion
  216.8 7.9 %all-to-all-done.5 = bf16[32,8,640]{2,1,0:T(8,128)(2,1)S(1)} async-done(((bf16[32,8,640]{2,1,0:T(8,128)(2,1)}), bf16[32,8,640]{2,1,0:T(8,128)(2,1)S(1)}, u32[]{:S(2)}, u32[]{:S(2)}) %all-to-all-start.5) | async-done | bytes 327712 | tf_op jit(solution)/shard_map/all_to_all | solution.py:343
  224.7 0.8 slice_add_fusion
  225.6 1.1 reshape.57.in_ref
  226.7 1.5 copy-done.1
  228.2 1.5 copy-done.3
  229.8 1.2 copy-done.7
  231.0 0.9 copy-done.13
  231.9 9.3 %grad.1 = (bf16[768,640]{1,0:T(8,128)(2,1)}, f32[10,768]{1,0:T(8,128)}) custom-call(f32[10,768]{1,0:T(8,128)S(1)} %copy-done.17, f32[10,1]{1,0:T(8,128)S(1)} %copy-done.21, bf16[768,640]{1,0:T(8,128)(2,1)S(1)} %copy-done.5, bf16[768,128]{1,0:T(8,128)(2,1)S(1)} %copy-done.10, bf16[768,128]{1,0:T(8,128)(2,1)S(1)} %copy-done.13, ...), custom_call_target="tpu_custom_call" | custom-call | flops 2000000000 | bytes 8388608 | tf_op jit(solution)/shard_map/grad/pallas_call | solution.py:404
  (76 shorter events, 3.3 us)
Async XLA Ops:
  7.2 95.9 %all-gather.4.cloned.1.call-start = ((), (), s32[]{:S(2)}) async-start(), calls=%async_computation.8 | async-start | bytes 3686400 | tf_op jit(solution)/shard_map/all_gather | solution.py:375
  20.9 1.2 copy-start.4
  22.1 0.9 copy-start.9
  23.0 0.8 copy-start.14
  23.8 4.0 %copy-start.18 = (f32[10,1]{1,0:T(8,128)}, f32[10,1]{1,0:T(8,128)S(1)}, u32[]{:S(2)}) copy-start(f32[10,1]{1,0:T(8,128)S(1)} %copy.63.alog_ref) | copy-start | bytes 124
  27.8 23.1 %copy-start.31 = (f32[6,128,640]{2,1,0:T(8,128)}, f32[6,128,640]{2,1,0:T(8,128)S(1)}, u32[]{:S(2)}) copy-start(f32[6,128,640]{2,1,0:T(8,128)S(1)} %get-tuple-element.16.inc_ref) | copy-start | bytes 5898244
  51.0 8.1 %copy-start.36 = (f32[10]{0:T(128)S(1)}, f32[10]{0:T(128)}, u32[]{:S(2)}) copy-start(f32[10]{0:T(128)} %param.16) | copy-start | bytes 124
  51.9 20.2 %copy-start.5 = (bf16[768,640]{1,0:T(8,128)(2,1)S(1)}, bf16[768,640]{1,0:T(8,128)(2,1)}, u32[]{:S(2)}) copy-start(bf16[768,640]{1,0:T(8,128)(2,1)} %x_ref.7) | copy-start | bytes 2949124
  51.9 20.2 %copy-start.10 = (bf16[768,128]{1,0:T(8,128)(2,1)S(1)}, bf16[768,128]{1,0:T(8,128)(2,1)}, u32[]{:S(2)}) copy-start(bf16[768,128]{1,0:T(8,128)(2,1)} %b_ref.5) | copy-start | bytes 589828
  51.9 19.9 %all-to-all-start.1 = ((bf16[32,8,640]{2,1,0:T(8,128)(2,1)}), bf16[32,8,640]{2,1,0:T(8,128)(2,1)S(1)}, u32[]{:S(2)}, u32[]{:S(2)}) async-start(bf16[32,8,640]{2,1,0:T(8,128)(2,1)} %scan_up.1), calls=%async_computation.1 | async-start | bytes 655360 | tf_op jit(solution)/shard_map/all_to_all | solution.py:343
  59.2 0.6 copy-start.34
  72.1 0.9 copy-start.11
  73.1 0.8 copy-start.15
  73.9 0.7 copy-start.19
  74.6 0.7 copy-start.22
  75.2 1.2 copy-start.28
  76.4 1.6 copy-start.32
  83.7 1.4 copy-start
  85.1 0.6 copy-start.26
  87.0 16.0 %all-to-all-start.2 = ((f32[8,1,768]{2,1,0:T(1,128)}), f32[8,1,768]{2,1,0:T(1,128)S(1)}, u32[]{:S(2)}, u32[]{:S(2)}) async-start(f32[8,1,768]{2,1,0:T(1,128)} %broadcast_in_dim.39), calls=%async_computation.2 | async-start | bytes 49152 | tf_op jit(solution)/shard_map/all_to_all | solution.py:362
  103.1 2.4 copy-start.29
  103.1 2.4 copy-start.35
  103.1 3.4 %copy-start.37 = (bf16[768,2560]{1,0:T(8,128)(2,1)S(1)}, bf16[768,2560]{1,0:T(8,128)(2,1)}, u32[]{:S(2)}) copy-start(bf16[768,2560]{1,0:T(8,128)(2,1)} %param.19) | copy-start | bytes 11796484
  111.6 11.4 %all-to-all-start.3 = ((f32[8,1,768]{2,1,0:T(1,128)}), f32[8,1,768]{2,1,0:T(1,128)S(1)}, u32[]{:S(2)}, u32[]{:S(2)}) async-start(f32[8,1,768]{2,1,0:T(1,128)} %broadcast_in_dim.40), calls=%async_computation.3 | async-start | bytes 49152 | tf_op jit(solution)/shard_map/all_to_all | solution.py:362
  123.1 43.7 %all-to-all-start.6 = ((bf16[4,640,640]{1,2,0:T(8,128)(2,1)}), bf16[4,640,640]{1,2,0:T(8,128)(2,1)}, u32[]{:S(2)}, u32[]{:S(2)}) async-start(bf16[4,640,640]{1,2,0:T(8,128)(2,1)} %bitcast.16), calls=%async_computation.6 | async-start | bytes 6553600 | tf_op jit(solution)/shard_map/all_to_all | solution.py:383
  129.0 0.9 copy-start.12
  129.9 0.8 copy-start.16
  130.7 0.7 copy-start.20
  131.4 0.7 copy-start.23
  132.0 0.7 copy-start.25
  132.7 0.7 copy-start.27
  133.4 1.2 copy-start.30
  134.6 1.2 copy-start.33
  141.6 1.3 copy-start.2
  142.9 0.9 copy-start.6
  166.8 15.3 %all-to-all-start.4 = ((bf16[32,8,640]{2,1,0:T(8,128)(2,1)}), bf16[32,8,640]{2,1,0:T(8,128)(2,1)S(1)}, u32[]{:S(2)}, u32[]{:S(2)}) async-start(bf16[32,8,640]{2,1,0:T(8,128)(2,1)} %pad_maximum_fusion.1), calls=%async_computation.4 | async-start | bytes 655360 | tf_op jit(solution)/shard_map/all_to_all | solution.py:401
  182.1 26.7 %all-to-all-start.7 = ((bf16[8,80,640]{2,1,0:T(8,128)(2,1)}), bf16[8,80,640]{2,1,0:T(8,128)(2,1)}, u32[]{:S(2)}, u32[]{:S(2)}) async-start(bf16[8,80,640]{2,1,0:T(8,128)(2,1)} %bitcast.20), calls=%async_computation.7 | async-start | bytes 1638400 | tf_op jit(solution)/shard_map/all_to_all | solution.py:385
  187.6 0.7 copy-start.8
  208.8 15.9 %all-to-all-start.5 = ((bf16[32,8,640]{2,1,0:T(8,128)(2,1)}), bf16[32,8,640]{2,1,0:T(8,128)(2,1)S(1)}, u32[]{:S(2)}, u32[]{:S(2)}) async-start(bf16[32,8,640]{2,1,0:T(8,128)(2,1)} %copy-done.8), calls=%async_computation.5 | async-start | bytes 655360 | tf_op jit(solution)/shard_map/all_to_all | solution.py:343
  214.8 11.9 %copy-start.17 = (f32[10,768]{1,0:T(8,128)S(1)}, f32[10,768]{1,0:T(8,128)}, u32[]{:S(2)}) copy-start(f32[10,768]{1,0:T(8,128)} %dt_ref.7) | copy-start | bytes 92164
  214.8 11.9 %copy-start.21 = (f32[10,1]{1,0:T(8,128)S(1)}, f32[10,1]{1,0:T(8,128)}, u32[]{:S(2)}) copy-start(f32[10,1]{1,0:T(8,128)} %copy-done.18) | copy-start | bytes 124
  214.8 11.9 %copy-start.24 = (f32[1,640]{1,0:T(1,128)S(1)}, f32[1,640]{1,0:T(1,128)}, u32[]{:S(2)}) copy-start(f32[1,640]{1,0:T(1,128)} %broadcast_in_dim_reshape.3.skip_ref) | copy-start | bytes 7684
  226.7 1.5 copy-start.1
  228.2 1.5 copy-start.3
  229.8 1.2 copy-start.7
  231.0 0.9 copy-start.13
Sparse Core Ops, SparseCore 0:
  20.2 64.1 all-gather.3
